TPU v7x, 256 devices: a whole 4x4x8 slice. The times are simulated.
256 devices in a mesh: ep: 16 (over z, core), fsdp: 4 (over x), tp: 4 (over y).
Axes of the slice: x: 4, y: 4, z: 8, core: 2. Of those that a mesh axis runs over, the one named last changes fastest.
Arguments:
- out_grad: bfloat16 [8192, 4096], P(('ep', 'fsdp')), may hold values from -1.5 to 1.5
- routes: int32 [8192, 2], P(('ep', 'fsdp')), may hold values from 0 to 15, all different within a row; in each aligned block of 128 rows (0 to 127, 128 to 255, ...) at most 32 rows name the same one
- chosen_logits: float32 [8192, 2], P(('ep', 'fsdp')), may hold values from -4 to 4
- routed_inputs: bfloat16 [16, 16, 4, 32, 4096], P('ep', None, 'fsdp'), may hold values from -6 to 6
- w_gate: bfloat16 [16, 4096, 1024], P('ep', 'fsdp', 'tp'), may hold values from -0.09375 to 0.09375
- w_up: bfloat16 [16, 4096, 1024], P('ep', 'fsdp', 'tp'), may hold values from -0.09375 to 0.09375
- w_down: bfloat16 [16, 1024, 4096], P('ep', 'tp', 'fsdp'), may hold values from -0.1875 to 0.1875
Outputs:
- input_grad: bfloat16 [8192, 4096], P(('ep', 'fsdp'))
- logit_grad: float32 [8192, 2], P(('ep', 'fsdp'))
- grad_gate: float32 [16, 4096, 1024], P('ep', 'fsdp', 'tp')
- grad_up: float32 [16, 4096, 1024], P('ep', 'fsdp', 'tp')
- grad_down: float32 [16, 1024, 4096], P('ep', 'tp', 'fsdp')
Inputs may be any that keep to these rules, and one draw needn't show every extreme that they name: Each row of routes names 2 different experts. In each token group of 128 consecutive rows no expert is named by more than 32 rows, a bound that some block reaches.
All inputs are finite; a program needn't handle non-finite values.
Results may differ from a plain program's by a relative error of at most 0.015.
Values may be sent and summed in bfloat16 or wider, within the bound.
A program may use at most 128 MiB of HBM per device.

v0:
```python
import jax
import jax.numpy as jnp
from jax import lax
from jax.sharding import PartitionSpec as P


def laid_out(parts, dim):
    shape = list(parts.shape[1:])
    shape[dim] *= parts.shape[0]
    return jnp.moveaxis(parts, 0, dim).reshape(shape)


def gather_together(arrays, axis, dims):
    ravelled = jnp.concatenate([a.reshape(-1) for a in arrays])
    lines, at, outs = (lax.all_gather(ravelled, axis), 0, [])
    for a, dim in zip(arrays, dims):
        parts = lines[:, at : at + a.size].reshape(-1, *a.shape)
        outs.append(laid_out(parts, dim))
        at += a.size
    return tuple(outs)


def own_rows(product, width, axis):
    whole = product(jnp.int32(0), width * lax.axis_size(axis)).astype(jnp.bfloat16)
    return lax.psum_scatter(whole, axis, scatter_dimension=0, tiled=True).astype(jnp.float32)


def slot_places(routes, experts, capacity):
    flat_routes = routes.reshape(-1)
    onehot = (flat_routes[:, None] == jnp.arange(experts, dtype=jnp.int32)[None, :]).astype(
        jnp.int32
    )
    earlier = (jnp.cumsum(onehot, axis=0) - onehot).astype(jnp.int32)
    position = jnp.sum(earlier * onehot, axis=1).astype(jnp.int32)
    return (flat_routes * capacity + position).astype(jnp.int32)


def weighted_rows(grad_rows, gate_probs):
    scaled = gate_probs[:, :, None] * grad_rows.astype(jnp.float32)[:, None, :]
    return scaled.astype(jnp.bfloat16).reshape(-1, grad_rows.shape[1])


def fill_slots(values, slot_index, total_slots):
    row_total = values.shape[0]
    source = jnp.full((total_slots,), row_total, jnp.int32)
    source = source.at[slot_index].set(jnp.arange(row_total, dtype=jnp.int32))
    padded = jnp.concatenate([values, jnp.zeros((1, values.shape[1]), values.dtype)], axis=0)
    return jnp.take(padded, source, axis=0)


def combine(returned, slot_index, tokens, per_token):
    picked = jnp.take(returned, slot_index, axis=0).astype(jnp.float32)
    return jnp.sum(picked.reshape(tokens, per_token, -1), axis=1).astype(jnp.bfloat16)


def transpose_dot(left, right):
    return lax.dot_general(
        left, right, (((0,), (0,)), ((), ())), preferred_element_type=jnp.float32
    )


def contract_last(left, right):
    return lax.dot_general(
        left, right, (((1,), (1,)), ((), ())), preferred_element_type=jnp.float32
    )


def on_device(out_grad, routes, chosen_logits, routed_inputs, w_gate, w_up, w_down):
    experts = lax.axis_size("ep")
    tp_count = lax.axis_size("tp")
    tokens, model_width = out_grad.shape
    per_token = routes.shape[1]
    capacity = routed_inputs.shape[3]
    gate_probs = jax.nn.softmax(chosen_logits, axis=-1)
    slot_index = slot_places(routes, experts, capacity)
    inputs = routed_inputs.reshape(-1, model_width)
    narrow = model_width // tp_count
    column_piece = lax.dynamic_slice_in_dim(out_grad, lax.axis_index("tp") * narrow, narrow, 1)
    outgoing = fill_slots(weighted_rows(column_piece, gate_probs), slot_index, experts * capacity)
    arrived = lax.all_to_all(
        outgoing.reshape(experts, capacity, narrow), "ep", split_axis=0, concat_axis=0, tiled=True
    )
    scaled = lax.all_gather(arrived.reshape(-1, narrow), "tp", axis=1, tiled=True)
    gate_full, up_full, down_full = gather_together((w_gate, w_up, w_down), "fsdp", (1, 1, 2))
    gate_full = gate_full[0]
    up_full = up_full[0]
    down_full = down_full[0]
    gate_act = jnp.dot(inputs, gate_full, preferred_element_type=jnp.float32)
    up_act = jnp.dot(inputs, up_full, preferred_element_type=jnp.float32)
    sigmoid_gate = jax.nn.sigmoid(gate_act)
    silu_gate = gate_act * sigmoid_gate
    hidden = (silu_gate * up_act).astype(jnp.bfloat16)
    hidden_grad = contract_last(scaled, down_full)
    products = jnp.sum(hidden_grad * hidden.astype(jnp.float32), axis=1)
    up_grad = (hidden_grad * silu_gate).astype(jnp.bfloat16)
    gate_grad = (
        hidden_grad * up_act * sigmoid_gate * (1.0 + gate_act * (1.0 - sigmoid_gate))
    ).astype(jnp.bfloat16)
    slot_part = contract_last(gate_grad, gate_full) + contract_last(up_grad, up_full)
    pair_grads = jnp.concatenate([gate_grad, up_grad], axis=1)

    def grad_term(first_row, row_count):
        input_cols = lax.dynamic_slice_in_dim(inputs, first_row, row_count, 1)
        scaled_cols = lax.dynamic_slice_in_dim(scaled, first_row, row_count, 1)
        gate_up_part = transpose_dot(input_cols, pair_grads)
        down_part = transpose_dot(scaled_cols, hidden)
        return jnp.concatenate([gate_up_part, down_part], axis=1)

    grad_rows = own_rows(grad_term, model_width // lax.axis_size("fsdp"), "fsdp")
    hidden_units = hidden.shape[1]
    grad_gate = grad_rows[:, :hidden_units][None]
    grad_up = grad_rows[:, hidden_units : 2 * hidden_units][None]
    grad_down = grad_rows[:, 2 * hidden_units :].T[None]
    narrow = model_width // tp_count
    column_sum = lax.psum_scatter(
        slot_part.astype(jnp.bfloat16), "tp", scatter_dimension=1, tiled=True
    ).astype(jnp.float32)
    product_sum = lax.psum(products.astype(jnp.bfloat16), "tp").astype(jnp.float32)
    leaving = (
        column_sum.astype(jnp.bfloat16).reshape(experts, capacity, narrow),
        product_sum.astype(jnp.bfloat16).reshape(experts, capacity),
    )
    back_rows, back_products = (
        lax.all_to_all(leaving[0], "ep", split_axis=0, concat_axis=0, tiled=True),
        lax.all_to_all(leaving[1], "ep", split_axis=0, concat_axis=0, tiled=True),
    )
    combined = combine(back_rows.reshape(-1, narrow), slot_index, tokens, per_token)
    input_grad = lax.all_gather(combined, "tp", axis=1, tiled=True)
    chosen = (
        jnp.take(back_products.reshape(-1), slot_index)
        .astype(jnp.float32)
        .reshape(tokens, per_token)
    )
    logit_grad = chosen - gate_probs * jnp.sum(chosen, axis=1, keepdims=True)
    return (input_grad, logit_grad, grad_gate, grad_up, grad_down)


def solution(mesh):
    return jax.shard_map(
        on_device,
        mesh=mesh,
        in_specs=(
            P(("ep", "fsdp"), None),
            P(("ep", "fsdp"), None),
            P(("ep", "fsdp"), None),
            P("ep", None, "fsdp", None, None),
            P("ep", "fsdp", "tp"),
            P("ep", "fsdp", "tp"),
            P("ep", "tp", "fsdp"),
        ),
        out_specs=(
            P(("ep", "fsdp"), None),
            P(("ep", "fsdp"), None),
            P("ep", "fsdp", "tp"),
            P("ep", "fsdp", "tp"),
            P("ep", "tp", "fsdp"),
        ),
        check_vma=False,
    )
```

profile of v0, /device:TPU:1, one launch (start us, length us, event | category | flops | bytes accessed | tf_op | source)
XLA Modules:
  0.0 340.7 jit_solution(7325050296816589945)
XLA Ops:
  7.2 1.5 copy.58
  8.7 1.5 copy.59
  10.1 1.1 copy.60
  11.3 1.2 pad_maximum_fusion.1
  13.0 1.0 dynamic-slice_convert_fusion
  14.0 0.4 mul.83
  14.4 0.7 mul.84
  15.5 0.6 reduce-window.6
  16.1 0.2 slice_reduce_fusion
  16.7 1.4 scatter_custom_fusion
  18.4 2.1 gather_fusion
  20.4 0.2 broadcast_select_fusion
  20.6 38.3 %all_to_all.19 = bf16[16,32,1024]{2,1,0:T(8,128)(2,1)} all-to-all(bf16[16,32,1024]{2,1,0:T(8,128)(2,1)S(1)} %broadcast_select_fusion), channel_id=1, replica_groups=mesh['ep'=16,'fsdp'=4,'tp'=4] {'ep'}, dimensions={0} | all-to-all | bytes 2097152 | tf_op jit(solution)/shard_map/all_to_all | solution.py:80
  58.9 0.2 reduce-scatter.3.cloned.1.call-start
  59.2 25.3 %all-gather.9.cloned.1.call-done = bf16[3145728]{0:T(1024)(128)(2,1)} async-done(((bf16[786432]{0:T(1024)(128)(2,1)}), bf16[3145728]{0:T(1024)(128)(2,1)}) %all-gather.9.cloned.1.call-update) | async-done | bytes 6291472 | tf_op jit(solution)/shard_map/all_gather | solution.py:15
  84.5 7.8 %reshape.171 = bf16[4,786432]{1,0:T(4,128)(2,1)} reshape(bf16[3145728]{0:T(1024)(128)(2,1)} %all-gather.9.cloned.1.call-done) | data formatting | bytes 12582912 | tf_op jit(solution)/shard_map/all_gather | solution.py:15
  92.3 5.4 %fusion.15 = (bf16[4,262144]{1,0:T(4,128)(2,1)}, bf16[4,262144]{1,0:T(4,128)(2,1)S(1)}, bf16[4,262144]{1,0:T(4,128)(2,1)}) fusion(bf16[4,786432]{1,0:T(4,128)(2,1)} %reshape.171), kind=kLoop, calls=%fused_computation.56 | loop fusion | bytes 12582912 | tf_op jit(solution)/shard_map/slice | solution.py:17
  97.6 3.3 squeeze_reshape_transpose_reshape.7
  100.9 3.7 %squeeze_reshape_transpose_reshape.6 = bf16[4096,256]{1,0:T(8,128)(2,1)S(1)} reshape(bf16[4,262144]{1,0:T(4,128)(2,1)} %get-tuple-element.34) | data formatting | bytes 4194304 | tf_op jit(solution)/shard_map/squeeze;reshape;transpose;reshape | solution.py:86
  104.6 3.6 %copy.64 = bf16[1,4,256,1024]{3,2,1,0:T(8,128)(2,1)} copy(bf16[1,4,256,1024]{3,1,2,0:T(4,128)(2,1)} %bitcast.71) | data formatting | bytes 4194304
  108.2 4.0 %copy.52 = bf16[1,256,4,1024]{1,3,2,0:T(8,128)(2,1)} copy(bf16[1,256,4,1024]{3,1,2,0:T(8,128)(2,1)} %bitcast.70) | data formatting | bytes 4194304 | tf_op jit(solution)/shard_map/transpose | solution.py:10
  112.1 4.3 %convolution_bitcast_fusion = f32[512,256]{0,1:T(8,128)S(1)} fusion(bf16[4096,256]{1,0:T(8,128)(2,1)} %squeeze_reshape_transpose_reshape.7, bf16[512,4096]{1,0:T(8,128)(2,1)} %bitcast.85), kind=kOutput, calls=%fused_computation.11 | convolution fusion | flops 1073741824 | bytes 6815744 | tf_op jit(solution)/shard_map/dot_general | solution.py:88
  116.5 2.1 convolution_bitcast_fusion.1
  118.6 19.2 %all-gather.5.cloned.1.call-done = bf16[512,4096]{1,0:T(8,128)(2,1)} async-done(((bf16[512,1024]{1,0:T(8,128)(2,1)}), bf16[512,4096]{1,0:T(8,128)(2,1)}) %all-gather.5.cloned.1.call-update) | async-done | bytes 4194320 | tf_op jit(solution)/shard_map/all_gather | solution.py:83
  137.8 4.5 %multiply_reduce_fusion = (bf16[512]{0:T(512)(128)(2,1)S(1)}, bf16[512,256]{0,1:T(8,128)(2,1)S(1)}, bf16[512,256]{0,1:T(8,128)(2,1)S(1)}, bf16[512,256]{0,1:T(8,128)(2,1)S(1)}) fusion(f32[512,256]{0,1:T(8,128)} %convolution_bitcast_fusion.1, f32[512,256]{0,1:T(8,128)S(1)} %convolution_bitcast_fusion, bf16[512,4096]{1,0:T(8,128)(2,1)} %all-gather.5.cloned.1.call-done, ...), kind=kOutput, calls=%fused_computation.23 | convolution fusion | flops 1076100608 | bytes 8127488 | tf_op jit(solution)/shard_map/dot_general | solution.py:63
  142.3 1.3 fusion.16
  143.7 3.4 add_convert_fusion
  147.1 6.6 %psum.7 = bf16[16,1,32]{2,0,1:T(8,128)(2,1)S(1)} all-reduce(bf16[16,1,32]{2,0,1:T(8,128)(2,1)S(1)} %all_to_all.14), channel_id=1, replica_groups=mesh['ep'=16,'fsdp'=4,'tp'=4] {'tp'}, use_global_device_ids=true, to_apply=%region_9.10 | all-reduce | flops 512 | bytes 2048 | tf_op jit(solution)/shard_map/psum | solution.py:118
  153.7 16.9 %all_to_all.20 = bf16[16,1,32]{2,1,0:T(2,128)(2,1)S(1)} all-to-all(bf16[16,1,32]{2,1,0:T(2,128)(2,1)S(1)} %copy.53), channel_id=1, replica_groups=mesh['ep'=16,'fsdp'=4,'tp'=4] {'ep'}, dimensions={0} | all-to-all | bytes 2048 | tf_op jit(solution)/shard_map/all_to_all | solution.py:125
  170.7 26.4 %reduce-scatter.3.cloned.1.call-done = bf16[512,1024]{1,0:T(8,128)(2,1)} async-done(((bf16[512,4096]{1,0:T(8,128)(2,1)}), bf16[512,1024]{1,0:T(8,128)(2,1)}) %reduce-scatter.3.cloned.1.call-update) | async-done | bytes 1048592 | tf_op jit(solution)/shard_map/reduce_scatter | solution.py:115
  197.1 7.7 %all-to-all-start.1 = ((bf16[16,32,1024]{2,1,0:T(8,128)(2,1)}), bf16[16,32,1024]{2,1,0:T(8,128)(2,1)S(1)}, u32[]{:S(2)}, u32[]{:S(2)}) async-start(bf16[16,32,1024]{2,1,0:T(8,128)(2,1)} %bitcast.78), calls=%async_computation.2 | async-start | bytes 2097152 | tf_op jit(solution)/shard_map/all_to_all | solution.py:124
  205.2 1.9 gather_fusion.2
  207.6 25.2 %all-to-all-done.1 = bf16[16,32,1024]{2,1,0:T(8,128)(2,1)S(1)} async-done(((bf16[16,32,1024]{2,1,0:T(8,128)(2,1)}), bf16[16,32,1024]{2,1,0:T(8,128)(2,1)S(1)}, u32[]{:S(2)}, u32[]{:S(2)}) %all-to-all-start.1) | async-done | bytes 1048608 | tf_op jit(solution)/shard_map/all_to_all | solution.py:124
  232.8 1.2 gather_fusion.1
  234.0 0.2 gather.21
  234.2 1.9 fusion.1
  236.1 0.3 reduce-scatter.5.cloned.1.call-start
  236.4 3.7 %convolution_convert_fusion.1 = bf16[4096,256]{0,1:T(8,128)(2,1)S(1)} fusion(bf16[512,256]{0,1:T(8,128)(2,1)S(1)} %get-tuple-element.33, bf16[512,4096]{1,0:T(8,128)(2,1)} %all-gather.5.cloned.1.call-done), kind=kOutput, calls=%fused_computation.8 | convolution fusion | flops 1074790400 | bytes 6553600 | tf_op jit(solution)/shard_map/dot_general | solution.py:57
  240.1 2.4 fusion
  242.5 3.4 %pad_maximum_fusion = bf16[4096,768]{0,1:T(8,128)(2,1)} fusion(bf16[4096,256]{0,1:T(8,128)(2,1)S(1)} %convolution_convert_fusion.1, bf16[4096,512]{0,1:T(8,128)(2,1)S(1)} %fusion), kind=kLoop, calls=%fused_computation.5 | loop fusion | flops 12582912 | bytes 12582912 | tf_op jit(solution)/shard_map/concatenate | solution.py:107
  245.9 0.6 convert_subtract_fusion
  246.5 9.8 %all-gather.7.cloned.1.call-done = bf16[128,4096]{1,0:T(8,128)(2,1)} async-done(((bf16[128,1024]{1,0:T(8,128)(2,1)}), bf16[128,4096]{1,0:T(8,128)(2,1)}) %all-gather.7.cloned.1.call-update) | async-done | bytes 1048592 | tf_op jit(solution)/shard_map/all_gather | solution.py:128
  256.3 71.3 %reduce-scatter.5.cloned.1.call-done = bf16[1024,768]{0,1:T(8,128)(2,1)} async-done(((bf16[4096,768]{0,1:T(8,128)(2,1)}), bf16[1024,768]{0,1:T(8,128)(2,1)}) %reduce-scatter.5.cloned.1.call-update) | async-done | bytes 1572880 | tf_op jit(solution)/shard_map/reduce_scatter | solution.py:25
  327.6 1.8 convert_element_type.58
  329.4 1.2 slice_bitcast_fusion
  330.6 1.3 copy.55
  331.9 1.3 copy.56
  333.2 1.0 copy.66
  (54 shorter events, 2.5 us)
Async XLA Ops:
  7.2 77.3 %all-gather.9.cloned.1.call-start = ((), (), s32[]{:S(2)}) async-start(), calls=%async_computation.9 | async-start | bytes 7864320 | tf_op jit(solution)/shard_map/all_gather | solution.py:15
  10.1 2.5 copy-start.3
  12.5 2.6 copy-start.2
  12.6 125.2 %all-gather.5.cloned.1.call-start = ((), (), s32[]{:S(2)}) async-start(), calls=%async_computation.5 | async-start | bytes 5242880 | tf_op jit(solution)/shard_map/all_gather | solution.py:83
  58.9 138.1 %reduce-scatter.3.cloned.1.call-start = ((), (), s32[]{:S(2)}) async-start(), calls=%async_computation.6 | async-start | bytes 5242880 | tf_op jit(solution)/shard_map/reduce_scatter | solution.py:115
  112.1 4.4 %copy-start.4 = (bf16[1,16,1,32,4096]{4,3,2,1,0:T(8,128)(2,1)S(1)}, bf16[1,16,1,32,4096]{4,3,2,1,0:T(8,128)(2,1)}, u32[]{:S(2)}) copy-start(bf16[1,16,1,32,4096]{4,3,2,1,0:T(8,128)(2,1)} %param.10) | copy-start | bytes 12582916
  137.8 4.5 %copy-start = (bf16[4096,256]{1,0:T(8,128)(2,1)S(1)}, bf16[4096,256]{1,0:T(8,128)(2,1)}, u32[]{:S(2)}) copy-start(bf16[4096,256]{1,0:T(8,128)(2,1)} %squeeze_reshape_transpose_reshape.7) | copy-start | bytes 6291460
  197.1 35.7 %all-to-all-start.1 = ((bf16[16,32,1024]{2,1,0:T(8,128)(2,1)}), bf16[16,32,1024]{2,1,0:T(8,128)(2,1)S(1)}, u32[]{:S(2)}, u32[]{:S(2)}) async-start(bf16[16,32,1024]{2,1,0:T(8,128)(2,1)} %bitcast.78), calls=%async_computation.2 | async-start | bytes 2097152 | tf_op jit(solution)/shard_map/all_to_all | solution.py:124
  204.8 51.5 %all-gather.7.cloned.1.call-start = ((), (), s32[]{:S(2)}) async-start(), calls=%async_computation.7 | async-start | bytes 1310720 | tf_op jit(solution)/shard_map/all_gather | solution.py:128
  236.1 91.6 %reduce-scatter.5.cloned.1.call-start = ((), (), s32[]{:S(2)}) async-start(), calls=%async_computation.8 | async-start | bytes 7864320 | tf_op jit(solution)/shard_map/reduce_scatter | solution.py:25
  236.4 3.7 %copy-start.5 = (bf16[1,16,1,32,4096]{4,3,2,1,0:T(8,128)(2,1)S(1)}, bf16[1,16,1,32,4096]{4,3,2,1,0:T(8,128)(2,1)}, u32[]{:S(2)}) copy-start(bf16[1,16,1,32,4096]{4,3,2,1,0:T(8,128)(2,1)} %param.10) | copy-start | bytes 12582916
  330.6 2.6 copy-start.1
Sparse Core Ops, SparseCore 0:
  12.7 71.7 all-gather.8
  86.3 51.4 all-gather.4
  147.2 49.8 reduce-scatter.2
  236.2 20.0 all-gather.6
  258.7 68.8 reduce-scatter.4
where the time goes:
time: 341 us
  waiting for transfers between devices  177 us (52%)
  blocking collectives  61.8 us (18%)
  local copies, waits for them, and re-layouts  46.3 us (14%)
  matrix products  21.7 us (6%)
  between operations  14.1 us (4%)
  other arithmetic  11.1 us (3%)
  starting transfers between devices  8.39 us (2%)
    reduce_scatter x1, waiting for transfers between devices, own_rows(): lax.psum_scatter(whole, axis, scatter_dimension=0, tiled=True)  71.3 us
    all_to_all x1, blocking collectives, on_device(): lax.all_to_all(outgoing.reshape(experts, capacity, narrow), 'ep', split_a...  38.3 us
    reduce_scatter x1, waiting for transfers between devices, on_device(): lax.psum_scatter(slot_part.astype(jnp.bfloat16), 'tp', scatter_dimension=...  26.4 us
    all_gather x1, waiting for transfers between devices, gather_together(): lines, at, outs = (lax.all_gather(ravelled, axis), 0, [])  25.3 us
    all_to_all x1, waiting for transfers between devices, on_device(): lax.all_to_all(leaving[0], 'ep', split_axis=0, concat_axis=0, tiled=True)  25.2 us
    all_gather x1, waiting for transfers between devices, on_device(): lax.all_gather(arrived.reshape(-1, narrow), 'tp', axis=1, tiled=True)  19.2 us
    all_to_all x1, blocking collectives, on_device(): lax.all_to_all(leaving[1], 'ep', split_axis=0, concat_axis=0, tiled=True)  16.9 us
    unnamed x20, local copies, waits for them, and re-layouts  11.3 us
  transfers between devices with their start and end apart: 6, of which 6 were waited for; matrix products, arithmetic and copies ran while one was open for 16% of the time, Pallas kernels for 0%

commit v1 on v0

--- a/solution.py
+++ b/solution.py
@@ -1,7 +1,18 @@
+import functools
 import jax
 import jax.numpy as jnp
 from jax import lax
 from jax.sharding import PartitionSpec as P
+
+
+def list_the_clusters(xx, axis_name):
+    mixed_arr = jnp.stack([xx for _ in range(lax.axis_size(axis_name))], axis=0)
+    long_array = lax.all_to_all(mixed_arr, axis_name, 0, 0)
+    carry = jnp.concatenate(long_array, 1)
+    return carry
+
+
+make_state = functools.partial(list_the_clusters, axis_name="tp")
 
 
 def laid_out(parts, dim):
@@ -80,7 +91,7 @@
     arrived = lax.all_to_all(
         outgoing.reshape(experts, capacity, narrow), "ep", split_axis=0, concat_axis=0, tiled=True
     )
-    scaled = lax.all_gather(arrived.reshape(-1, narrow), "tp", axis=1, tiled=True)
+    scaled = make_state(arrived.reshape(-1, narrow))
     gate_full, up_full, down_full = gather_together((w_gate, w_up, w_down), "fsdp", (1, 1, 2))
     gate_full = gate_full[0]
     up_full = up_full[0]

time: 341 us -> 322 us (0.944)
  waiting for transfers between devices: 177 us -> 149 us
  starting transfers between devices: 8.39 us -> 13.3 us
    all_gather x1 -> x0, waiting for transfers between devices: 19.2 us -> none  [on_device(): lax.all_gather(arrived.reshape(-1, narrow), 'tp', axis=1, tiled=True)]
    all_gather x1, waiting for transfers between devices: 25.3 us -> 17.8 us  [gather_together(): lines, at, outs = (lax.all_gather(ravelled, axis), 0, [])]
    all_to_all x0 -> x1, starting transfers between devices: none -> 4.94 us  [list_the_clusters(): long_array = lax.all_to_all(mixed_arr, axis_name, 0, 0)]
  transfers between devices with their start and end apart: 6 -> 6, of which waited for: 6 -> 5; matrix products, arithmetic and copies ran while one was open for 16% -> 18% of each run, Pallas kernels for 0% -> 0%
where the time goes in v1:
time: 322 us
  waiting for transfers between devices  149 us (46%)
  blocking collectives  63.4 us (20%)
  local copies, waits for them, and re-layouts  48.9 us (15%)
  matrix products  21.7 us (7%)
  between operations  14.1 us (4%)
  starting transfers between devices  13.3 us (4%)
  other arithmetic  11.1 us (3%)
    reduce_scatter x1, waiting for transfers between devices, own_rows(): lax.psum_scatter(whole, axis, scatter_dimension=0, tiled=True)  71.3 us
    all_to_all x1, blocking collectives, on_device(): lax.all_to_all(outgoing.reshape(experts, capacity, narrow), 'ep', split_a...  38.2 us
    all_to_all x1, waiting for transfers between devices, on_device(): lax.all_to_all(leaving[0], 'ep', split_axis=0, concat_axis=0, tiled=True)  25.2 us
    reduce_scatter x1, waiting for transfers between devices, on_device(): lax.psum_scatter(slot_part.astype(jnp.bfloat16), 'tp', scatter_dimension=...  25.1 us
    all_gather x1, waiting for transfers between devices, gather_together(): lines, at, outs = (lax.all_gather(ravelled, axis), 0, [])  17.8 us
    all_to_all x1, blocking collectives, on_device(): lax.all_to_all(leaving[1], 'ep', split_axis=0, concat_axis=0, tiled=True)  16.7 us
    unnamed x20, local copies, waits for them, and re-layouts  11.3 us
    all_gather x1, waiting for transfers between devices, on_device(): input_grad = lax.all_gather(combined, 'tp', axis=1, tiled=True)  9.73 us
  transfers between devices with their start and end apart: 6, of which 5 were waited for; matrix products, arithmetic and copies ran while one was open for 18% of the time, Pallas kernels for 0%

profile of v1, /device:TPU:1, one launch (start us, length us, event | category | flops | bytes accessed | tf_op | source)
XLA Modules:
  0.0 321.6 jit_solution(8286597631055667036)
XLA Ops:
  7.2 1.5 copy.62
  8.7 1.5 copy.63
  10.1 1.1 copy.64
  11.3 1.2 pad_maximum_fusion.1
  13.0 1.0 dynamic-slice_convert_fusion
  14.0 0.4 mul.83
  14.3 0.7 mul.84
  15.4 0.6 reduce-window.6
  16.6 1.4 scatter_custom_fusion
  18.3 2.1 gather_fusion
  20.5 38.2 %all_to_all.24 = bf16[16,32,1024]{2,1,0:T(8,128)(2,1)S(1)} all-to-all(bf16[16,32,1024]{2,1,0:T(8,128)(2,1)S(1)} %broadcast_select_fusion), channel_id=1, replica_groups=mesh['ep'=16,'fsdp'=4,'tp'=4] {'ep'}, dimensions={0} | all-to-all | bytes 2097152 | tf_op jit(solution)/shard_map/all_to_all | solution.py:91
  58.8 0.5 copy.55
  59.3 2.3 stack.3
  61.6 4.9 %all-to-all-start.1 = ((bf16[4,512,1024]{1,2,0:T(8,128)(2,1)}), bf16[4,512,1024]{1,2,0:T(8,128)(2,1)}, u32[]{:S(2)}, u32[]{:S(2)}) async-start(bf16[4,512,1024]{1,2,0:T(8,128)(2,1)} %stack.3), calls=%async_computation.1 | async-start | bytes 8388608 | tf_op jit(solution)/shard_map/all_to_all | solution.py:10
  66.5 0.2 reduce-scatter.3.cloned.1.call-start
  66.7 17.8 %all-gather.6.cloned.1.call-done = bf16[3145728]{0:T(1024)(128)(2,1)} async-done(((bf16[786432]{0:T(1024)(128)(2,1)}), bf16[3145728]{0:T(1024)(128)(2,1)}) %all-gather.6.cloned.1.call-update) | async-done | bytes 6291472 | tf_op jit(solution)/shard_map/all_gather | solution.py:26
  84.5 7.8 %reshape.177 = bf16[4,786432]{1,0:T(4,128)(2,1)} reshape(bf16[3145728]{0:T(1024)(128)(2,1)} %all-gather.6.cloned.1.call-done) | data formatting | bytes 12582912 | tf_op jit(solution)/shard_map/all_gather | solution.py:26
  92.3 5.4 %fusion.15 = (bf16[4,262144]{1,0:T(4,128)(2,1)}, bf16[4,262144]{1,0:T(4,128)(2,1)S(1)}, bf16[4,262144]{1,0:T(4,128)(2,1)}) fusion(bf16[4,786432]{1,0:T(4,128)(2,1)} %reshape.177), kind=kLoop, calls=%fused_computation.56 | loop fusion | bytes 12582912 | tf_op jit(solution)/shard_map/slice | solution.py:28
  97.6 3.3 %squeeze_reshape_transpose_reshape.7 = bf16[4096,256]{1,0:T(8,128)(2,1)} reshape(bf16[4,262144]{1,0:T(4,128)(2,1)S(1)} %get-tuple-element.35) | data formatting | bytes 4194304 | tf_op jit(solution)/shard_map/squeeze;reshape;transpose;reshape | solution.py:96
  100.9 3.5 %squeeze_reshape_transpose_reshape.6 = bf16[4096,256]{1,0:T(8,128)(2,1)S(1)} reshape(bf16[4,262144]{1,0:T(4,128)(2,1)} %get-tuple-element.34) | data formatting | bytes 4194304 | tf_op jit(solution)/shard_map/squeeze;reshape;transpose;reshape | solution.py:97
  104.4 3.6 %copy.68 = bf16[1,4,256,1024]{3,2,1,0:T(8,128)(2,1)} copy(bf16[1,4,256,1024]{3,1,2,0:T(4,128)(2,1)} %bitcast.74) | data formatting | bytes 4194304
  108.0 3.9 %copy.56 = bf16[1,256,4,1024]{1,3,2,0:T(8,128)(2,1)} copy(bf16[1,256,4,1024]{3,1,2,0:T(8,128)(2,1)} %bitcast.73) | data formatting | bytes 4194304 | tf_op jit(solution)/shard_map/transpose | solution.py:21
  111.9 4.3 %convolution_bitcast_fusion = f32[512,256]{0,1:T(8,128)S(1)} fusion(bf16[4096,256]{1,0:T(8,128)(2,1)} %squeeze_reshape_transpose_reshape.7, bf16[512,4096]{1,0:T(8,128)(2,1)} %bitcast.88), kind=kOutput, calls=%fused_computation.11 | convolution fusion | flops 1073741824 | bytes 6815744 | tf_op jit(solution)/shard_map/dot_general | solution.py:99
  116.2 2.1 convolution_bitcast_fusion.1
  118.3 4.5 %multiply_reduce_fusion = (bf16[512]{0:T(512)(128)(2,1)S(1)}, bf16[512,256]{0,1:T(8,128)(2,1)S(1)}, bf16[512,256]{0,1:T(8,128)(2,1)S(1)}, bf16[512,256]{0,1:T(8,128)(2,1)S(1)}) fusion(f32[512,256]{0,1:T(8,128)} %convolution_bitcast_fusion.1, f32[512,256]{0,1:T(8,128)S(1)} %convolution_bitcast_fusion, bf16[512,4096]{0,1:T(8,128)(2,1)} %bitcast.6, ...), kind=kOutput, calls=%fused_computation.23 | convolution fusion | flops 1076100608 | bytes 8127488 | tf_op jit(solution)/shard_map/dot_general | solution.py:74
  122.9 1.3 fusion.16
  124.2 3.4 %add_convert_fusion = bf16[512,4096]{1,0:T(8,128)(2,1)} fusion(f32[512,4096]{1,0:T(8,128)S(1)} %fusion.16, bf16[512,256]{0,1:T(8,128)(2,1)S(1)} %get-tuple-element.41, bf16[4096,256]{1,0:T(8,128)(2,1)S(1)} %squeeze_reshape_transpose_reshape.6), kind=kOutput, calls=%fused_computation.4 | convolution fusion | flops 1077936128 | bytes 14942208 | tf_op jit(solution)/shard_map/dot_general | solution.py:74
  127.6 8.4 %psum.7 = bf16[16,1,32]{2,0,1:T(8,128)(2,1)S(1)} all-reduce(bf16[16,1,32]{2,0,1:T(8,128)(2,1)S(1)} %all_to_all.18), channel_id=1, replica_groups=mesh['ep'=16,'fsdp'=4,'tp'=4] {'tp'}, use_global_device_ids=true, to_apply=%region_9.10 | all-reduce | flops 512 | bytes 2048 | tf_op jit(solution)/shard_map/psum | solution.py:129
  136.1 16.7 %all_to_all.25 = bf16[16,1,32]{2,1,0:T(2,128)(2,1)S(1)} all-to-all(bf16[16,1,32]{2,1,0:T(2,128)(2,1)S(1)} %copy.57), channel_id=1, replica_groups=mesh['ep'=16,'fsdp'=4,'tp'=4] {'ep'}, dimensions={0} | all-to-all | bytes 2048 | tf_op jit(solution)/shard_map/all_to_all | solution.py:136
  152.8 25.1 %reduce-scatter.3.cloned.1.call-done = bf16[512,1024]{1,0:T(8,128)(2,1)} async-done(((bf16[512,4096]{1,0:T(8,128)(2,1)}), bf16[512,1024]{1,0:T(8,128)(2,1)}) %reduce-scatter.3.cloned.1.call-update) | async-done | bytes 1048592 | tf_op jit(solution)/shard_map/reduce_scatter | solution.py:126
  177.9 7.8 %all-to-all-start.2 = ((bf16[16,32,1024]{2,1,0:T(8,128)(2,1)}), bf16[16,32,1024]{2,1,0:T(8,128)(2,1)S(1)}, u32[]{:S(2)}, u32[]{:S(2)}) async-start(bf16[16,32,1024]{2,1,0:T(8,128)(2,1)} %bitcast.81), calls=%async_computation.3 | async-start | bytes 2097152 | tf_op jit(solution)/shard_map/all_to_all | solution.py:135
  186.1 1.9 gather_fusion.2
  188.4 25.2 %all-to-all-done.2 = bf16[16,32,1024]{2,1,0:T(8,128)(2,1)S(1)} async-done(((bf16[16,32,1024]{2,1,0:T(8,128)(2,1)}), bf16[16,32,1024]{2,1,0:T(8,128)(2,1)S(1)}, u32[]{:S(2)}, u32[]{:S(2)}) %all-to-all-start.2) | async-done | bytes 1048608 | tf_op jit(solution)/shard_map/all_to_all | solution.py:135
  213.7 1.2 gather_fusion.1
  214.8 0.2 gather.21
  215.1 1.9 fusion.1
  216.9 0.3 reduce-scatter.5.cloned.1.call-start
  217.3 3.7 %convolution_convert_fusion.1 = bf16[4096,256]{0,1:T(8,128)(2,1)S(1)} fusion(bf16[512,4096]{0,1:T(8,128)(2,1)} %bitcast.6, bf16[512,256]{0,1:T(8,128)(2,1)S(1)} %get-tuple-element.33), kind=kOutput, calls=%fused_computation.8 | convolution fusion | flops 1074790400 | bytes 6553600 | tf_op jit(solution)/shard_map/dot_general | solution.py:68
  221.0 2.4 fusion
  223.4 3.4 %pad_maximum_fusion = bf16[4096,768]{0,1:T(8,128)(2,1)} fusion(bf16[4096,256]{0,1:T(8,128)(2,1)S(1)} %convolution_convert_fusion.1, bf16[4096,512]{0,1:T(8,128)(2,1)S(1)} %fusion), kind=kLoop, calls=%fused_computation.5 | loop fusion | flops 12582912 | bytes 12582912 | tf_op jit(solution)/shard_map/concatenate | solution.py:118
  226.9 0.6 convert_subtract_fusion
  227.4 9.7 %all-gather.4.cloned.1.call-done = bf16[128,4096]{1,0:T(8,128)(2,1)} async-done(((bf16[128,1024]{1,0:T(8,128)(2,1)}), bf16[128,4096]{1,0:T(8,128)(2,1)}) %all-gather.4.cloned.1.call-update) | async-done | bytes 1048592 | tf_op jit(solution)/shard_map/all_gather | solution.py:139
  237.2 71.3 %reduce-scatter.5.cloned.1.call-done = bf16[1024,768]{0,1:T(8,128)(2,1)} async-done(((bf16[4096,768]{0,1:T(8,128)(2,1)}), bf16[1024,768]{0,1:T(8,128)(2,1)}) %reduce-scatter.5.cloned.1.call-update) | async-done | bytes 1572880 | tf_op jit(solution)/shard_map/reduce_scatter | solution.py:36
  308.5 1.8 convert_element_type.58
  310.3 1.2 slice_bitcast_fusion
  311.5 1.3 copy.59
  312.8 1.3 copy.60
  314.1 1.0 copy.70
  (55 shorter events, 2.7 us)
Async XLA Ops:
  7.2 77.3 %all-gather.6.cloned.1.call-start = ((), (), s32[]{:S(2)}) async-start(), calls=%async_computation.9 | async-start | bytes 7864320 | tf_op jit(solution)/shard_map/all_gather | solution.py:26
  10.1 2.4 copy-start.3
  12.5 2.5 copy-start.2
  61.6 56.8 %all-to-all-start.1 = ((bf16[4,512,1024]{1,2,0:T(8,128)(2,1)}), bf16[4,512,1024]{1,2,0:T(8,128)(2,1)}, u32[]{:S(2)}, u32[]{:S(2)}) async-start(bf16[4,512,1024]{1,2,0:T(8,128)(2,1)} %stack.3), calls=%async_computation.1 | async-start | bytes 8388608 | tf_op jit(solution)/shard_map/all_to_all | solution.py:10
  66.5 111.4 %reduce-scatter.3.cloned.1.call-start = ((), (), s32[]{:S(2)}) async-start(), calls=%async_computation.6 | async-start | bytes 5242880 | tf_op jit(solution)/shard_map/reduce_scatter | solution.py:126
  111.9 4.3 %copy-start.4 = (bf16[1,16,1,32,4096]{4,3,2,1,0:T(8,128)(2,1)S(1)}, bf16[1,16,1,32,4096]{4,3,2,1,0:T(8,128)(2,1)}, u32[]{:S(2)}) copy-start(bf16[1,16,1,32,4096]{4,3,2,1,0:T(8,128)(2,1)} %param.10) | copy-start | bytes 12582916
  118.3 4.5 %copy-start = (bf16[4096,256]{1,0:T(8,128)(2,1)S(1)}, bf16[4096,256]{1,0:T(8,128)(2,1)}, u32[]{:S(2)}) copy-start(bf16[4096,256]{1,0:T(8,128)(2,1)} %squeeze_reshape_transpose_reshape.7) | copy-start | bytes 6291460
  177.9 35.8 %all-to-all-start.2 = ((bf16[16,32,1024]{2,1,0:T(8,128)(2,1)}), bf16[16,32,1024]{2,1,0:T(8,128)(2,1)S(1)}, u32[]{:S(2)}, u32[]{:S(2)}) async-start(bf16[16,32,1024]{2,1,0:T(8,128)(2,1)} %bitcast.81), calls=%async_computation.3 | async-start | bytes 2097152 | tf_op jit(solution)/shard_map/all_to_all | solution.py:135
  185.7 51.5 %all-gather.4.cloned.1.call-start = ((), (), s32[]{:S(2)}) async-start(), calls=%async_computation.7 | async-start | bytes 1310720 | tf_op jit(solution)/shard_map/all_gather | solution.py:139
  216.9 91.6 %reduce-scatter.5.cloned.1.call-start = ((), (), s32[]{:S(2)}) async-start(), calls=%async_computation.8 | async-start | bytes 7864320 | tf_op jit(solution)/shard_map/reduce_scatter | solution.py:36
  217.2 3.7 %copy-start.5 = (bf16[1,16,1,32,4096]{4,3,2,1,0:T(8,128)(2,1)S(1)}, bf16[1,16,1,32,4096]{4,3,2,1,0:T(8,128)(2,1)}, u32[]{:S(2)}) copy-start(bf16[1,16,1,32,4096]{4,3,2,1,0:T(8,128)(2,1)} %param.10) | copy-start | bytes 12582916
  311.5 2.6 copy-start.1
Sparse Core Ops, SparseCore 0:
  12.7 71.7 all-gather.5
  127.7 50.1 reduce-scatter.2
  217.1 20.0 all-gather.3
  239.6 68.8 reduce-scatter.4
